TPU v7x, 32 devices: a whole 2x2x4 slice. The times are simulated.
32 devices in a mesh: dp: 4 (over x, core), tensor: 8 (over z, y).
Axes of the slice: x: 2, y: 2, z: 4, core: 2. Of those that a mesh axis runs over, the one named last changes fastest.
Arguments:
- hidden: bfloat16 [8, 64, 4608], P('dp', 'tensor'), may hold values from -6 to 6
- gain: float32 [4608], replicated, may hold values from 0.5 to 1.5
- labels: int32 [8, 64], P('dp', 'tensor'), may hold values from 0 to 255999
- lengths: int32 [8], replicated, may hold values from 1 to 64
- embed: bfloat16 [256000, 4608], P(('dp', 'tensor')), may hold values from -0.375 to 0.375
Outputs:
- token_logprob: float32 [8, 64], P('dp', 'tensor')
- mean_nll: float32 [], replicated
- z_loss: float32 [], replicated
All inputs are finite; a program needn't handle non-finite values.
Results may differ from a plain program's by a relative error of at most 0.00058.
Values may be sent and summed in bfloat16 or wider, within the bound.
A program may use at most 128 MiB of HBM per device.

v0:
```python
import jax
import jax.numpy as jnp
from jax import lax
from jax.sharding import PartitionSpec as P

CAP = 30


def normalize(rows, gain):
    values = rows.astype(jnp.float32)
    meansq = jnp.mean(values * values, axis=-1, keepdims=True)
    return (values * lax.rsqrt(meansq + 1e-06) * gain).astype(jnp.bfloat16)


def per_device(hidden, gain, labels, lengths, embed):
    n_tensor = lax.axis_size("tensor")
    n_all = lax.axis_size("dp") * n_tensor
    seqs, stretch, width = hidden.shape
    vocab_dev = embed.shape[0]
    rows_local = seqs * stretch
    total_rows = rows_local * n_all
    flat = hidden.reshape(rows_local, width)
    row_ids = jnp.arange(total_rows)
    owner = row_ids // rows_local
    within = row_ids % rows_local
    batch_ids = owner // n_tensor * seqs + within // stretch
    positions = owner % n_tensor * stretch + within % stretch
    live_all = (positions < jnp.take(lengths, batch_ids)).astype(jnp.float32)
    all_labels = lax.all_gather(labels.reshape(rows_local), ("dp", "tensor"), axis=0, tiled=True)
    outgoing = normalize(flat, gain)
    rows = lax.all_gather(outgoing, ("dp", "tensor"), axis=0, tiled=True)
    values = lax.dot_general(
        rows, embed, (((1,), (1,)), ((), ())), preferred_element_type=jnp.float32
    )
    capped = CAP * jnp.tanh(values / CAP)
    sumexp = jnp.sum(jnp.exp(capped), axis=1)
    first = lax.axis_index(("dp", "tensor")) * vocab_dev
    local = all_labels - first
    inside = (local >= 0) & (local < vocab_dev)
    chosen = jnp.take_along_axis(capped, jnp.clip(local, 0, vocab_dev - 1)[:, None], axis=1)[:, 0]
    picked = jnp.where(inside, chosen, jnp.float32(0.0))
    own_start = lax.axis_index(("dp", "tensor")) * rows_local
    sum_total, pick_total = lax.psum((sumexp, picked), ("dp", "tensor"))
    own_sum = lax.dynamic_slice_in_dim(sum_total, own_start, rows_local)
    own_pick = lax.dynamic_slice_in_dim(pick_total, own_start, rows_local)
    own_live = lax.dynamic_slice_in_dim(live_all, own_start, rows_local)
    lse = jnp.log(own_sum)
    token = own_live * (own_pick - lse)
    nll_sum, count, square_sum = lax.psum(
        (-jnp.sum(token), jnp.sum(own_live), jnp.sum(own_live * lse * lse)), ("dp", "tensor")
    )
    mean_nll = nll_sum / count
    z_loss = 0.01 * square_sum / count
    return (token.reshape(seqs, stretch), mean_nll, z_loss)


def solution(mesh):
    return jax.shard_map(
        per_device,
        mesh=mesh,
        in_specs=(P("dp", "tensor", None), P(), P("dp", "tensor"), P(), P(("dp", "tensor"), None)),
        out_specs=(P("dp", "tensor"), P(), P()),
        check_vma=False,
    )
```

profile of v0, /device:TPU:0, one launch (start us, length us, event | category | flops | bytes accessed | tf_op | source)
XLA Modules:
  0.0 241.1 jit_solution(1555822703838976775)
XLA Ops:
  7.2 0.0 all-gather.2.cloned.1.call-start
  7.2 1.0 fusion.3
  8.3 0.1 rsqrt.12
  8.3 1.7 fusion.2
  10.0 0.0 all-gather.2.cloned.1.call-update
  10.0 0.8 reshape.263
  10.8 0.2 dynamic-update-slice
  11.0 42.2 %all-reduce = s32[512]{0:T(512)S(1)} all-reduce(s32[512]{0:T(512)S(1)} %dynamic-update-slice), channel_id=1, replica_groups=mesh['dp'=4,'tensor'=8] {'dp','tensor'}, use_global_device_ids=true, to_apply=%add | all-reduce | flops 512 | bytes 4096
  53.2 1.6 fusion.29
  54.8 4.5 %compare_select_fusion.1 = s32[512,1]{0,1:T(1,128)S(1)} fusion(s32[]{:T(128)} %bitcast.1, s32[]{:T(128)} %bitcast.2, s32[]{:T(128)} %bitcast.3, s32[]{:T(128)} %bitcast.4, s32[]{:T(128)} %bitcast.5, s32[]{:T(128)} %bitcast.7, s32[]{:T(128)} %bitcast.6), kind=kLoop, calls=%fused_computation.11 | loop fusion | flops 30208 | bytes 2076 | tf_op jit(solution)/shard_map/jit(_take)/gather | solution.py:28
  59.4 0.7 fusion.26
  60.1 17.2 %all-gather.2.cloned.1.call-done = bf16[512,4608]{1,0:T(8,128)(2,1)} async-done(((bf16[16,4608]{1,0:T(8,128)(2,1)}), bf16[512,4608]{1,0:T(8,128)(2,1)}) %all-gather.2.cloned.1.call-update) | async-done | bytes 4718608 | tf_op jit(solution)/shard_map/all_gather | solution.py:31
  77.3 48.5 %exponential_reduce_fusion = (f32[512]{0:T(512)S(1)}, f32[512,8000]{0,1:T(8,128)}) fusion(bf16[512,4608]{1,0:T(8,128)(2,1)} %all-gather.2.cloned.1.call-done, bf16[8000,4608]{1,0:T(8,128)(2,1)} %param.9), kind=kOutput, calls=%fused_computation.1 | convolution fusion | flops 37761024000 | bytes 94832640 | tf_op jit(solution)/shard_map/dot_general | solution.py:32
  125.8 22.5 %gather_fusion = f32[512]{0:T(512)S(1)} fusion(f32[512,8000]{0,1:T(8,128)} %get-tuple-element.23, s32[512]{0:T(512)S(1)} %bitcast.23), kind=kCustom, calls=%fused_computation | custom fusion | bytes 8192 | tf_op jit(solution)/shard_map/jit(take_along_axis)/gather | solution.py:40
  148.3 38.1 %all-reduce.2 = (f32[512]{0:T(512)S(1)}, f32[512]{0:T(512)S(1)}) all-reduce(f32[512]{0:T(512)S(1)} %select_select_fusion.1, f32[512]{0:T(512)S(1)} %get-tuple-element.22), channel_id=1, replica_groups=mesh['dp'=4,'tensor'=8] {'dp','tensor'}, use_global_device_ids=true, to_apply=%region_1.2 | all-reduce | flops 1024 | bytes 8192 | tf_op jit(solution)/shard_map/psum | solution.py:43
  186.5 0.8 fusion.27
  187.2 0.6 reshape.216
  188.6 40.9 %all-reduce.1 = (f32[]{:T(128)}, f32[]{:T(128)}, f32[]{:T(128)}) all-reduce(f32[]{:T(128)S(6)} %neg.3, f32[]{:T(128)} %get-tuple-element.4, f32[]{:T(128)} %get-tuple-element.3), channel_id=1, replica_groups=mesh['dp'=4,'tensor'=8] {'dp','tensor'}, use_global_device_ids=true, to_apply=%region_5.6 | all-reduce | flops 3 | bytes 24 | tf_op jit(solution)/shard_map/psum | solution.py:49
  (8 shorter events, 0.1 us)
Async XLA Ops:
  7.2 70.1 %all-gather.2.cloned.1.call-start = ((), (), s32[]{:S(2)}) async-start(), calls=%async_computation | async-start | bytes 4866048 | tf_op jit(solution)/shard_map/all_gather | solution.py:31
Sparse Core Ops, SparseCore 0:
  10.9 66.3 all-gather.1
where the time goes:
time: 242 us; the launch traced here: 241 us
  blocking collectives  121 us (50%)
  matrix products  48.5 us (20%)
  local copies, waits for them, and re-layouts  25.8 us (11%)
  between operations  19.6 us (8%)
  waiting for transfers between devices  17.2 us (7%)
  other arithmetic  8.75 us (4%)
    dot_general x1, matrix products, per_device(): lax.dot_general(rows, embed, (((1,), (1,)), ((), ())), preferred_element_...  48.5 us
    unnamed x1, blocking collectives  42.2 us
    psum x1, blocking collectives, per_device(): lax.psum((-jnp.sum(token), jnp.sum(own_live), jnp.sum(own_live * lse * ls...  40.9 us
    psum x1, blocking collectives, per_device(): sum_total, pick_total = lax.psum((sumexp, picked), ('dp', 'tensor'))  38.1 us
    gather x1, local copies, waits for them, and re-layouts, per_device(): jnp.take_along_axis(capped, jnp.clip(local, 0, vocab_dev - 1)[:, None], a...  22.5 us
    all_gather x1, waiting for transfers between devices, per_device(): rows = lax.all_gather(outgoing, ('dp', 'tensor'), axis=0, tiled=True)  17.2 us
  transfers between devices with their start and end apart: 1, of which 1 were waited for; matrix products, arithmetic and copies ran while one was open for 3% of the time, Pallas kernels for 0%

commit v1 on v0

v1 whole, which is shorter than its diff:
```python
import functools
import math

import jax
import jax.numpy as jnp
from jax import lax
from jax.experimental import pallas as pl
from jax.experimental.pallas import tpu as pltpu
from jax.sharding import PartitionSpec as P

CAP = 30
LANES = 128
CHUNK = 256
MESH = pl.DeviceIdType.MESH


def tile_rows(vocab_dev):
    best = 16
    for size in range(16, 513, 16):
        if vocab_dev % size == 0:
            best = size
    return best


def kernel(
    cfg, hidden_ref, gain_ref, labels_ref, lengths_ref, embed_ref, out_ref,
    rows, tiles, acc0, acc1, sums, picks, labs, labrow, labels_all, mine, parts,
    tile_sem, ring_send, ring_recv, mate_send, mate_recv, lab_send, lab_recv, fin_send, fin_recv,
):
    n_dp, n_t, half, seqs, stretch, vt, n_tiles, n_slots, last, early = cfg
    n_all = n_dp * n_t
    chips = n_all // 2
    passes = chips * 2 * half // CHUNK
    per_pass = CHUNK // half
    dp, tt = lax.axis_index("dp"), lax.axis_index("tensor")
    me = dp * n_t + tt
    core = lax.rem(dp, 2)

    def swap(i):
        return i + lax.rem(i // 2, 2) * (1 - 2 * lax.rem(i, 2))

    def ring_of(x, t):
        q = swap(t)
        odd = lax.rem(x, 2)
        return x * n_t + q + odd * (n_t - 1 - 2 * q)

    def chip_of(r):
        x = r // n_t
        q = lax.rem(r, n_t)
        odd = lax.rem(x, 2)
        return x, swap(q + odd * (n_t - 1 - 2 * q))

    here = ring_of(dp // 2, tt)
    next_x, next_t = chip_of(lax.rem(here + 1 - 2 * core + chips, chips))
    next_dev = {"dp": next_x * 2 + core, "tensor": next_t}
    mate_dev = {"dp": dp + 1 - 2 * core, "tensor": tt}
    reach = last - core
    mate_reach = last - 1 + core

    def slot_of(d, side):
        return jnp.where(d == 0, 0, 2 * d - 1 + side)

    def block(slot, h):
        return rows.at[pl.ds(pl.multiple_of((slot * 2 + h) * half, half), half), :]

    def to_next(d, h):
        return pltpu.make_async_remote_copy(
            src_ref=block(slot_of(d, core), h), dst_ref=block(slot_of(d + 1, core), h),
            send_sem=ring_send.at[d, h], recv_sem=ring_recv.at[d + 1, h],
            device_id=next_dev, device_id_type=MESH)

    def from_last(d, h):
        return pltpu.make_async_remote_copy(
            src_ref=block(slot_of(d, core), h), dst_ref=block(slot_of(d, core), h),
            send_sem=ring_send.at[d, h], recv_sem=ring_recv.at[d, h],
            device_id=next_dev, device_id_type=MESH)

    def to_mate(d, h):
        return pltpu.make_async_remote_copy(
            src_ref=block(slot_of(d, core), h), dst_ref=block(slot_of(d, core), h),
            send_sem=mate_send.at[d, h], recv_sem=mate_recv.at[d, h],
            device_id=mate_dev, device_id_type=MESH)

    def from_mate(d, h):
        return pltpu.make_async_remote_copy(
            src_ref=block(slot_of(d, 1 - core), h), dst_ref=block(slot_of(d, 1 - core), h),
            send_sem=mate_send.at[d, h], recv_sem=mate_recv.at[d, h],
            device_id=mate_dev, device_id_type=MESH)

    def fetch(t):
        slot = lax.rem(t, n_slots)
        return pltpu.make_async_copy(
            embed_ref.at[pl.ds(pl.multiple_of(t * vt, vt), vt), :], tiles.at[slot], tile_sem.at[slot])

    def label_copy(source, target):
        return pltpu.make_async_remote_copy(
            src_ref=labels_ref, dst_ref=labels_all.at[source],
            send_sem=lab_send.at[target], recv_sem=lab_recv.at[source],
            device_id={"dp": target // n_t, "tensor": lax.rem(target, n_t)}, device_id_type=MESH)

    def part_copy(source, target):
        return pltpu.make_async_remote_copy(
            src_ref=mine, dst_ref=parts.at[source],
            send_sem=fin_send.at[target], recv_sem=fin_recv.at[source],
            device_id={"dp": target // n_t, "tensor": lax.rem(target, n_t)}, device_id_type=MESH)

    def others(visit):
        def body(k, carry):
            visit(lax.rem(me + k, n_all))
            return carry
        lax.fori_loop(1, n_all, body, 0)

    values = hidden_ref[...].astype(jnp.float32)
    meansq = jnp.mean(values * values, axis=-1, keepdims=True)
    rows[pl.ds(pl.multiple_of(core * half, half), half), :] = (
        values * lax.rsqrt(meansq + 1e-06) * gain_ref[...]).astype(jnp.bfloat16)

    barrier = pltpu.get_barrier_semaphore()
    others(lambda j: pl.semaphore_signal(
        barrier, inc=1, device_id={"dp": j // n_t, "tensor": lax.rem(j, n_t)}, device_id_type=MESH))

    def first_fetch(t, carry):
        fetch(t).start()
        return carry
    lax.fori_loop(0, n_slots, first_fetch, 0)

    sums[...] = jnp.zeros_like(sums)
    picks[...] = jnp.zeros_like(picks)
    acc1[...] = jnp.zeros_like(acc1)
    labels_all[me] = labels_ref[...]
    pl.semaphore_wait(barrier, n_all - 1)

    to_next(0, core).start()
    to_mate(0, core).start()
    others(lambda j: label_copy(me, j).start())
    from_mate(0, 1 - core).wait_recv()
    to_next(0, 1 - core).start()

    def ring_step(step):
        d = step // 2 + 1
        h = lax.rem(core + lax.rem(step, 2), 2)

        @pl.when(d <= reach)
        def _():
            from_last(d, h).wait_recv()
            to_mate(d, h).start()

            @pl.when(d < reach)
            def _():
                to_next(d, h).start()

    def ring_body(step, carry):
        ring_step(step)
        return carry

    def mate_body(step, carry):
        d = step // 2 + 1

        @pl.when(d <= mate_reach)
        def _():
            from_mate(d, lax.rem(core + 1 + lax.rem(step, 2), 2)).wait_recv()
        return carry

    lax.fori_loop(0, 2 * early, ring_body, 0)

    others(lambda j: label_copy(j, me).wait_recv())
    lane = lax.broadcasted_iota(jnp.int32, (1, LANES), 1)
    group = LANES // half

    def device_at(index):
        slot = index // 2
        d = (slot + 1) // 2
        away = jnp.where(lax.rem(slot, 2) == 1, chips - d, d)
        x, t = chip_of(lax.rem(here + away, chips))
        return (x * 2 + lax.rem(index, 2)) * n_t + t

    def place_labels(row, carry):
        total = jnp.zeros((1, LANES), jnp.int32)
        for b in range(group):
            total = jnp.where(lane // half == b, labels_all[device_at(row * group + b)], total)
        labrow[row] = total
        return carry
    lax.fori_loop(0, passes * CHUNK // LANES, place_labels, 0)
    for p in range(passes):
        labs[p] = jnp.concatenate([labrow[p * (CHUNK // LANES) + i] for i in range(CHUNK // LANES)], axis=1)

    lax.fori_loop(0, 2 * early, mate_body, 0)

    first = me * (vt * n_tiles)
    late = 2 * (last - early)

    def where_of(v):
        p = v // n_tiles
        q = lax.rem(v, n_tiles)
        odd = lax.rem(p, 2)
        return p, q, jnp.where(odd == 1, n_tiles - 1 - q, q)

    def score(acc, p, slot, t):
        th = jnp.tanh(acc[...] * (1.0 / CAP))
        grown = jnp.exp2(th * (CAP * math.log2(math.e)))
        local = labs[p] - (first + t * vt)
        chosen = jnp.where(lax.broadcasted_iota(jnp.int32, (vt, CHUNK), 0) == local, th, 0.0)
        sums[slot] += jnp.sum(grown.reshape(vt // 8, 8, CHUNK), axis=0)
        picks[slot] += jnp.sum(chosen.reshape(vt // 8, 8, CHUNK), axis=0)

    def visit(v, acc, before):
        p, q, t = where_of(v)
        slot = lax.rem(t, n_slots)

        @pl.when((v < n_tiles) | (q >= n_slots))
        def _():
            fetch(t).wait()

        if late > 0:
            @pl.when((v < n_tiles) & (lax.rem(v, 2) == 1) & (v // 2 < late))
            def _():
                ring_step(2 * early + v // 2)

            @pl.when(v == n_tiles)
            def _():
                lax.fori_loop(2 * early, 2 * last, mate_body, 0)

        @pl.when((v > 0) & (lax.rem(v - 1, n_tiles) + n_slots < n_tiles))
        def _():
            _, _, used = where_of(v - 1)
            odd = lax.rem((v - 1) // n_tiles, 2)
            fetch(used + n_slots - 2 * odd * n_slots).start()

        product = lax.dot_general(
            tiles[slot], rows[pl.ds(pl.multiple_of(p * CHUNK, CHUNK), CHUNK), :],
            (((1,), (1,)), ((), ())), preferred_element_type=jnp.float32)
        vb = jnp.maximum(v - 1, 0)
        pb, _, tb = where_of(vb)
        score(before, pb, jnp.where(v == 0, passes, pb), tb)
        acc[...] = product

    def pair(i, carry):
        visit(2 * i, acc0, acc1)
        visit(2 * i + 1, acc1, acc0)
        return carry
    lax.fori_loop(0, passes * n_tiles // 2, pair, 0)
    end = passes * n_tiles - 1
    p_end, _, t_end = where_of(jnp.int32(end))
    score(acc1, p_end, p_end, t_end)

    n_rows = passes * CHUNK // LANES
    for p in range(passes):
        total = jnp.sum(sums[p], axis=0, keepdims=True)
        chosen = jnp.sum(picks[p], axis=0, keepdims=True)
        for i in range(CHUNK // LANES):
            row = p * (CHUNK // LANES) + i
            labrow_f = total[:, i * LANES:(i + 1) * LANES]
            pick_f = chosen[:, i * LANES:(i + 1) * LANES]
            parts[n_all + row, 0:1, :] = labrow_f
            parts[n_all + row, 1:2, :] = pick_f

    for row in range(n_rows):
        total = jnp.zeros((2, LANES), jnp.float32)
        for b in range(group):
            dev = row * group + b
            x, t = (dev // n_t) // 2, jnp.int32(dev % n_t)
            side = (dev // n_t) % 2
            ahead = lax.rem(ring_of(jnp.int32(x), t) - here + chips, chips)
            slot = jnp.where(ahead == 0, 0, jnp.where(ahead < last, 2 * ahead, 2 * (chips - ahead) - 1))
            index = slot * 2 + side
            shift = lax.rem(b - lax.rem(index, group) + group, group) * half
            held = parts[n_all + index // group]
            total = jnp.where(lane // half == b, pltpu.roll(held, shift, 1)[0:2], total)
        mine[row:row + 1, :] = total[0:1]
        mine[n_rows + row:n_rows + row + 1, :] = total[1:2]

    parts[me, 0:2 * n_rows, :] = mine[...]
    others(lambda j: part_copy(me, j).start())
    others(lambda j: part_copy(j, me).wait_recv())

    def add_part(j, carry):
        return carry + parts[j, 0:2 * n_rows, :]
    total = lax.fori_loop(0, n_all, add_part, jnp.zeros((2 * n_rows, LANES), jnp.float32))
    lse = jnp.log(total[0:n_rows])
    picked = total[n_rows:2 * n_rows] * CAP
    spot = lax.broadcasted_iota(jnp.int32, (n_rows, LANES), 0) * LANES + lax.broadcasted_iota(
        jnp.int32, (n_rows, LANES), 1)
    owner, within = spot // half, lax.rem(spot, half)
    batch = owner // n_t * seqs + within // stretch
    position = lax.rem(owner, n_t) * stretch + lax.rem(within, stretch)
    limit = jnp.zeros((n_rows, LANES), jnp.int32)
    for b in range(n_dp * seqs):
        limit = jnp.where(batch == b, lengths_ref[b], limit)
    live = jnp.where((position < limit) & (within < seqs * stretch), 1.0, 0.0)
    token = live * (picked - lse)

    def whole(x):
        return jnp.sum(jnp.sum(x, axis=1, keepdims=True), axis=0, keepdims=True)
    count = whole(live)
    nll = -whole(token) / count
    z_loss = 0.01 * whole(live * lse * lse) / count
    mine_token = jnp.zeros((1, LANES), jnp.float32)
    for row in range(n_rows):
        mine_token = jnp.where(me // group == row, token[row:row + 1], mine_token)
    shift = lax.rem(group - lax.rem(me, group), group) * half
    out_ref[...] = jnp.zeros_like(out_ref)
    out_ref[...] = pltpu.roll(jnp.broadcast_to(mine_token, (8, LANES)), shift, 1)
    out_ref[1:2, :] = jnp.broadcast_to(nll, (1, LANES))
    out_ref[2:3, :] = jnp.broadcast_to(z_loss, (1, LANES))

    def drain(step, carry):
        d = step // 2
        h = lax.rem(step, 2)

        @pl.when(d < reach)
        def _():
            to_next(d, h).wait_send()

        @pl.when((d <= reach) & ((d > 0) | (h == core)))
        def _():
            to_mate(d, h).wait_send()
        return carry
    lax.fori_loop(0, 2 * (last + 1), drain, 0)
    others(lambda j: label_copy(me, j).wait_send())
    others(lambda j: part_copy(me, j).wait_send())


def solution(mesh):
    n_dp, n_t = mesh.shape["dp"], mesh.shape["tensor"]

    def per_device(hidden, gain, labels, lengths, embed):
        seqs, stretch, width = hidden.shape
        n_all = n_dp * n_t
        rows_local = seqs * stretch
        half = 16 * pl.cdiv(rows_local, 16)
        vocab_dev = embed.shape[0]
        vt = tile_rows(vocab_dev)
        n_tiles = vocab_dev // vt
        total = n_all * half
        passes = total // CHUNK
        n_slots = min(n_tiles, (56 * 1024 * 1024 - total * width * 2) // (vt * width * 2))
        chips = n_all // 2
        last = chips // 2
        early = min(last, pl.cdiv(CHUNK // (2 * half), 2))
        if passes != 2 or 2 * (last - early) > n_tiles // 2:
            early = last
        n_rows = total // LANES
        flat = jnp.pad(hidden.reshape(rows_local, width), ((0, half - rows_local), (0, 0)))
        own = jnp.pad(labels.reshape(1, rows_local), ((0, 0), (0, half - rows_local)), constant_values=-1)
        own = jnp.tile(own, (1, LANES // half))
        cfg = (n_dp, n_t, half, seqs, stretch, vt, n_tiles, n_slots, last, early)
        vmem = pl.BlockSpec(memory_space=pltpu.VMEM)
        dma = pltpu.SemaphoreType.DMA
        part_rows = max(8, 2 * n_rows)
        out = pl.pallas_call(
            functools.partial(kernel, cfg),
            out_shape=jax.ShapeDtypeStruct((8, LANES), jnp.float32),
            in_specs=[vmem, vmem, vmem, pl.BlockSpec(memory_space=pltpu.SMEM), pl.BlockSpec(memory_space=pl.ANY)],
            out_specs=vmem,
            scratch_shapes=[
                pltpu.VMEM((total, width), jnp.bfloat16),
                pltpu.VMEM((n_slots, vt, width), jnp.bfloat16),
                pltpu.VMEM((vt, CHUNK), jnp.float32),
                pltpu.VMEM((vt, CHUNK), jnp.float32),
                pltpu.VMEM((passes + 1, 8, CHUNK), jnp.float32),
                pltpu.VMEM((passes + 1, 8, CHUNK), jnp.float32),
                pltpu.VMEM((passes, 1, CHUNK), jnp.int32),
                pltpu.VMEM((n_rows, 1, LANES), jnp.int32),
                pltpu.VMEM((n_all, 1, LANES), jnp.int32),
                pltpu.VMEM((2 * n_rows, LANES), jnp.float32),
                pltpu.VMEM((n_all + n_rows, part_rows, LANES), jnp.float32),
                dma((n_slots,)),
                dma((last + 1, 2)), dma((last + 1, 2)), dma((last + 1, 2)), dma((last + 1, 2)),
                dma((n_all,)), dma((n_all,)), dma((n_all,)), dma((n_all,)),
            ],
            compiler_params=pltpu.CompilerParams(
                collective_id=0, has_side_effects=True, vmem_limit_bytes=67043328),
        )(flat, gain.reshape(1, width), own, lengths, embed)
        return out[0, :rows_local].reshape(seqs, stretch), out[1, 0], out[2, 0]

    return jax.shard_map(
        per_device,
        mesh=mesh,
        in_specs=(P("dp", "tensor", None), P(), P("dp", "tensor"), P(), P(("dp", "tensor"), None)),
        out_specs=(P("dp", "tensor"), P(), P()),
        check_vma=False,
    )
```

time: 242 us -> 129 us (0.53)
  Pallas kernels: 0 us -> 123 us
  blocking collectives: 121 us -> 0 us
  matrix products: 48.5 us -> 0 us
  local copies, waits for them, and re-layouts: 25.8 us -> 5.29 us
  between operations: 19.6 us -> 0.64 us
  waiting for transfers between devices: 17.2 us -> 0 us
  other arithmetic: 8.75 us -> 0 us
    pallas_call x0 -> x1, Pallas kernels: none -> 123 us  [per_device(): pl.pallas_call(functools.partial(kernel, cfg), out_shape=jax.ShapeDtypeSt...]
    psum x2 -> x0, blocking collectives: 79.1 us -> none  [the longest x1 40.9 us: per_device(): lax.psum((-jnp.sum(token), jnp.sum(own_live), jnp.sum(own_live * lse * ls...]
    dot_general x1 -> x0, matrix products: 48.5 us -> none  [per_device(): lax.dot_general(rows, embed, (((1,), (1,)), ((), ())), preferred_element_...]
    unnamed x1 -> x0, blocking collectives: 42.2 us -> none
    gather x2 -> x0, local copies, waits for them, and re-layouts: 24.1 us -> none  [the longest x1 22.5 us: per_device(): jnp.take_along_axis(capped, jnp.clip(local, 0, vocab_dev - 1)[:, None], a...]
    all_gather x1 -> x0, waiting for transfers between devices: 17.2 us -> none  [per_device(): rows = lax.all_gather(outgoing, ('dp', 'tensor'), axis=0, tiled=True)]
    gather x4 -> x0, other arithmetic: 4.58 us -> none  [the longest x2 4.56 us: per_device(): live_all = (positions < jnp.take(lengths, batch_ids)).astype(jnp.float32)]
  transfers between devices with their start and end apart: 1 -> 0, of which waited for: 1 -> 0; matrix products, arithmetic and copies ran while one was open for 3% -> 0% of each run, Pallas kernels for 0% -> 0%
where the time goes in v1:
time: 129 us
  Pallas kernels  123 us (95%)
  local copies, waits for them, and re-layouts  5.29 us (4%)
    pallas_call x1, Pallas kernels, per_device(): pl.pallas_call(functools.partial(kernel, cfg), out_shape=jax.ShapeDtypeSt...  123 us

profile of v1, /device:TPU:0, one launch (start us, length us, event | category | flops | bytes accessed | tf_op | source)
XLA Modules:
  0.0 129.0 jit_solution(13955901061496308562)
XLA Ops:
  0.6 0.8 tile.11
  1.4 0.6 tile.13.labels_ref
  2.0 1.3 %reshape.21.gain_ref = f32[1,4608]{1,0:T(1,128)} reshape(f32[4608]{0:T(1024)} %param.6) | data formatting | bytes 36864 | tf_op jit(solution)/shard_map/reshape | solution.py:373
  3.3 123.1 %shard_map.76 = f32[8,128]{1,0:T(8,128)} custom-call(bf16[16,4608]{1,0:T(8,128)(2,1)} %bitcast.3, f32[1,4608]{1,0:T(1,128)} %reshape.21.gain_ref, s32[1,128]{1,0:T(1,128)} %tile.13.labels_ref, s32[8]{0:T(128)} %lengths_ref.1, bf16[8000,4608]{1,0:T(8,128)(2,1)} %embed_ref.1), custom_call_target="tpu_custom_call" | custom-call | tf_op jit(solution)/shard_map/pallas_call | solution.py:350
  126.4 0.7 slice_reduce_fusion
  127.1 1.3 fusion
  128.4 0.6 reshape_squeeze.3
  (1 shorter events, 0.0 us)
